TPU v7x, 32 devices: a whole 2x2x4 slice. The times are simulated.
32 devices in a mesh: gx: 8 (over z, y), gy: 2 (over x), ha: 2 (over core).
Axes of the slice: x: 2, y: 2, z: 4, core: 2. Of those that a mesh axis runs over, the one named last changes fastest.
Arguments:
- coupling: bfloat16 [8, 4, 4, 768, 768], P('gx', ('gy', 'ha')), may hold values from -0.125 to 0.125
- interior_inverse: bfloat16 [8, 4, 4, 768, 768], P('gx', ('gy', 'ha')), as said below
- boundary_stiffness: bfloat16 [8, 4, 768, 768], P('gx', ('gy', 'ha')), as said below
- block_counts: int32 [8, 4], P('gx', ('gy', 'ha')), may hold values from 1 to 4, as said below
- initial_traces: float32 [8, 4, 768, 128], P('gx', ('gy', 'ha')), may hold values from -2 to 2
- trace_loads: float32 [8, 4, 768, 128], P('gx', ('gy', 'ha')), may hold values from -18 to 18
Outputs:
- traces: float32 [8, 4, 768, 128], P('gx', ('gy', 'ha'))
- residual: float32 [8, 4, 768, 128], P('gx', ('gy', 'ha'))
Inputs may be any that keep to these rules, and one draw needn't show every extreme that they name: `block_counts`: the two cells in columns 2m and 2m+1 of one grid row hold at most 5 blocks together; some cell holds 4. `interior_inverse`: symmetric in its last two dimensions. `boundary_stiffness`: symmetric in its last two dimensions.
All inputs are finite; a program needn't handle non-finite values.
Results may differ from a plain program's by a relative error of at most 0.00095.
Values may be sent and summed in bfloat16 or wider, within the bound.
A program may use at most 128 MiB of HBM per device.

v0:
```python
import jax
import jax.numpy as jnp
from jax import lax
from jax.sharding import PartitionSpec as P

SWEEPS = 3


penalty_weight = 2.0
lower_bound = 1.0
upper_bound = 14.0
spectrum_centre = (upper_bound + lower_bound) / 2.0
spectrum_half = (upper_bound - lower_bound) / 2.0
sigma_ratio = spectrum_centre / spectrum_half


def from_behind(block, axis, distance):
    devices = range(lax.axis_size(axis))
    route = [(i - distance, i) for i in devices if i - distance in devices]
    return lax.ppermute(block, axis, route)


def schur_block(coupling_block, inverse_block):
    product = jnp.dot(coupling_block, inverse_block, preferred_element_type=jnp.float32).astype(
        jnp.bfloat16
    )
    return jnp.dot(product, coupling_block.T, preferred_element_type=jnp.float32)


def apply_operator(condensed, traces):
    trace_width, load_width = traces.shape
    mode_width = trace_width // 6
    coupled = jnp.dot(
        condensed, traces, precision=lax.Precision.HIGHEST, preferred_element_type=jnp.float32
    )
    face_traces = traces.reshape(6, mode_width, load_width)
    from_below_x = from_behind(face_traces[1], "gx", 1)
    from_above_x = from_behind(face_traces[0], "gx", -1)
    from_below_y = from_behind(face_traces[3], ("gy", "ha"), 1)
    from_above_y = from_behind(face_traces[2], ("gy", "ha"), -1)
    absent = jnp.zeros_like(from_below_x)
    neighbours = jnp.stack(
        [from_below_x, from_above_x, from_below_y, from_above_y, absent, absent], 0
    )
    neighbours = neighbours.reshape(trace_width, load_width)
    return coupled + penalty_weight * (traces - neighbours)


def on_device(
    coupling, interior_inverse, boundary_stiffness, block_counts, initial_traces, trace_loads
):
    blocks = block_counts[0, 0]
    own_coupling = coupling[0, 0]
    own_inverse = interior_inverse[0, 0]
    slot_total = own_coupling.shape[0]
    trace_width = own_coupling.shape[1]
    empty = jnp.zeros((trace_width, trace_width), jnp.float32)
    condensed = boundary_stiffness[0, 0].astype(jnp.float32)
    for slot_index in range(slot_total):
        term = lax.cond(
            blocks > slot_index,
            lambda: schur_block(own_coupling[slot_index], own_inverse[slot_index]),
            lambda: empty,
        )
        condensed = condensed - term
    loads_local = trace_loads[0, 0]
    traces = initial_traces[0, 0]
    residual = loads_local - apply_operator(condensed, traces)
    direction = residual / spectrum_centre
    weight_old = 1.0 / sigma_ratio
    for sweep_index in range(SWEEPS):
        traces = traces + direction
        residual = loads_local - apply_operator(condensed, traces)
        if sweep_index + 1 < SWEEPS:
            weight_new = 1.0 / (2.0 * sigma_ratio - weight_old)
            direction = (
                weight_new * weight_old * direction + 2.0 * weight_new / spectrum_half * residual
            )
            weight_old = weight_new
    return (traces[None, None], residual[None, None])


def solution(mesh):
    in_specs = (
        P("gx", ("gy", "ha"), None, None, None),
        P("gx", ("gy", "ha"), None, None, None),
        P("gx", ("gy", "ha"), None, None),
        P("gx", ("gy", "ha")),
        P("gx", ("gy", "ha"), None, None),
        P("gx", ("gy", "ha"), None, None),
    )
    out_specs = (P("gx", ("gy", "ha"), None, None), P("gx", ("gy", "ha"), None, None))
    return jax.shard_map(
        on_device, mesh=mesh, in_specs=in_specs, out_specs=out_specs, check_vma=False
    )
```

profile of v0, /device:TPU:25, one launch (start us, length us, event | category | flops | bytes accessed | tf_op | source)
XLA Modules:
  0.0 95.5 jit_solution(14544788068167286450)
XLA Ops:
  2.3 3.1 %collective-permute-start = (f32[128,128]{1,0:T(8,128)}, f32[128,128]{1,0:T(8,128)}, u32[]{:S(2)}, u32[]{:S(2)}) collective-permute-start(f32[128,128]{1,0:T(8,128)} %get-tuple-element.52), channel_id=1, source_target_pairs={{0,4},{4,8},{8,12},{12,16},{16,20},{20,24},{24,28},{1,5},{5,9},{9,... | collective-permute-start | bytes 196616 | tf_op jit(solution)/shard_map/ppermute | solution.py:20
  5.4 3.0 %collective-permute-start.1 = (f32[128,128]{1,0:T(8,128)}, f32[128,128]{1,0:T(8,128)}, u32[]{:S(2)}, u32[]{:S(2)}) collective-permute-start(f32[128,128]{1,0:T(8,128)} %get-tuple-element.51), channel_id=1, source_target_pairs={{4,0},{8,4},{12,8},{16,12},{20,16},{24,20},{28,24},{5,1},{9,5},{13... | collective-permute-start | bytes 196616 | tf_op jit(solution)/shard_map/ppermute | solution.py:20
  8.4 4.2 %collective-permute-start.2 = (f32[128,128]{1,0:T(8,128)}, f32[128,128]{1,0:T(8,128)}, u32[]{:S(2)}, u32[]{:S(2)}) collective-permute-start(f32[128,128]{1,0:T(8,128)} %get-tuple-element.53), channel_id=1, source_target_pairs={{0,1},{1,2},{2,3},{4,5},{5,6},{6,7},{8,9},{9,10},{10,11},{12,13},{... | collective-permute-start | bytes 196616 | tf_op jit(solution)/shard_map/ppermute | solution.py:20
  15.3 4.1 %conditional.4 = (f32[768,768]{1,0:T(8,128)S(1)}) conditional(s32[]{:T(128)} %bitcast.11, () %tuple.32, (bf16[4,768,768]{2,1,0:T(8,128)(2,1)}, bf16[4,768,768]{2,1,0:T(8,128)(2,1)}) %tuple.64), branch_computations={%region_0.0_spmd, %region_1.0_spmd} | conditional | flops 1812529152 | bytes 5898248 | solution.py:60
  15.3 4.1 %fusion.1 = f32[768,768]{1,0:T(8,128)S(1)} fusion(bf16[4,768,768]{2,1,0:T(8,128)(2,1)} %get-tuple-element.24, bf16[4,768,768]{2,1,0:T(8,128)(2,1)} %get-tuple-element.26), kind=kOutput, calls=%fused_computation.2 | convolution fusion | flops 1812529152 | bytes 5898240 | tf_op jit(solution)/shard_map/cond/branch_1_fun/dot_general | solution.py:27
  19.4 5.5 %conditional.5 = (f32[768,768]{1,0:T(8,128)}) conditional(s32[]{:T(128)} %bitcast.14, () %tuple.34, (bf16[4,768,768]{2,1,0:T(8,128)(2,1)}, bf16[4,768,768]{2,1,0:T(8,128)(2,1)}) %tuple.65), branch_computations={%region_2.0_spmd, %region_3.0_spmd} | conditional | flops 1812529152 | bytes 5898248 | solution.py:60
  19.4 5.5 %fusion.12 = f32[768,768]{1,0:T(8,128)} fusion(bf16[4,768,768]{2,1,0:T(8,128)(2,1)} %get-tuple-element.27, bf16[4,768,768]{2,1,0:T(8,128)(2,1)} %get-tuple-element.28), kind=kOutput, calls=%fused_computation.10 | convolution fusion | flops 1812529152 | bytes 5898240 | tf_op jit(solution)/shard_map/cond/branch_1_fun/dot_general | solution.py:27
  24.9 5.5 %conditional.6 = (f32[768,768]{1,0:T(8,128)}) conditional(s32[]{:T(128)} %bitcast.15, () %tuple.35, (bf16[4,768,768]{2,1,0:T(8,128)(2,1)}, bf16[4,768,768]{2,1,0:T(8,128)(2,1)}) %tuple.66), branch_computations={%region_4.0_spmd, %region_5.0_spmd} | conditional | flops 1812529152 | bytes 5898248 | solution.py:60
  24.9 5.5 %fusion.23 = f32[768,768]{1,0:T(8,128)} fusion(bf16[4,768,768]{2,1,0:T(8,128)(2,1)} %get-tuple-element.32, bf16[4,768,768]{2,1,0:T(8,128)(2,1)} %get-tuple-element.33), kind=kOutput, calls=%fused_computation.18 | convolution fusion | flops 1812529152 | bytes 5898240 | tf_op jit(solution)/shard_map/cond/branch_1_fun/dot_general | solution.py:27
  32.2 3.8 %fusion.46 = f32[768,768]{1,0:T(8,128)S(1)} fusion(f32[768,768]{1,0:T(8,128)} %get-tuple-element.61, f32[768,768]{1,0:T(8,128)} %get-tuple-element.60, f32[768,768]{1,0:T(8,128)} %get-tuple-element.59, f32[768,768]{1,0:T(8,128)S(1)} %get-tuple-element.58, bf16[1,1,768,768]{3,2,1,0:T(8,128)(2,1)S(1)} %copy-done.3), kind=kLoop, calls=%fused_computation.35 | loop fusion | flops 2949120 | bytes 12976128 | tf_op jit(solution)/shard_map/sub | solution.py:65
  41.6 2.8 %collective-permute-start.4 = (f32[128,128]{1,0:T(8,128)S(1)}, f32[128,128]{1,0:T(8,128)S(1)}, u32[]{:S(2)}, u32[]{:S(2)}) collective-permute-start(f32[128,128]{1,0:T(8,128)S(1)} %get-tuple-element.49), channel_id=1, source_target_pairs={{0,4},{4,8},{8,12},{12,16},{16,20},{20,24},{24,28},{1,5},{5,9},{9,... | collective-permute-start | bytes 196616 | tf_op jit(solution)/shard_map/ppermute | solution.py:20
  44.5 3.3 %collective-permute-start.5 = (f32[128,128]{1,0:T(8,128)S(1)}, f32[128,128]{1,0:T(8,128)S(1)}, u32[]{:S(2)}, u32[]{:S(2)}) collective-permute-start(f32[128,128]{1,0:T(8,128)S(1)} %get-tuple-element.48), channel_id=1, source_target_pairs={{4,0},{8,4},{12,8},{16,12},{20,16},{24,20},{28,24},{5,1},{9,5},{13... | collective-permute-start | bytes 196616 | tf_op jit(solution)/shard_map/ppermute | solution.py:20
  47.8 6.4 %collective-permute-start.6 = (f32[128,128]{1,0:T(8,128)S(1)}, f32[128,128]{1,0:T(8,128)S(1)}, u32[]{:S(2)}, u32[]{:S(2)}) collective-permute-start(f32[128,128]{1,0:T(8,128)S(1)} %get-tuple-element.47), channel_id=1, source_target_pairs={{0,1},{1,2},{2,3},{4,5},{5,6},{6,7},{8,9},{9,10},{10,11},{12,13},{... | collective-permute-start | bytes 196616 | tf_op jit(solution)/shard_map/ppermute | solution.py:20
  54.2 2.1 %collective-permute-start.7 = (f32[128,128]{1,0:T(8,128)S(1)}, f32[128,128]{1,0:T(8,128)S(1)}, u32[]{:S(2)}, u32[]{:S(2)}) collective-permute-start(f32[128,128]{1,0:T(8,128)S(1)} %get-tuple-element.46), channel_id=1, source_target_pairs={{1,0},{2,1},{3,2},{5,4},{6,5},{7,6},{9,8},{10,9},{11,10},{13,12},{... | collective-permute-start | bytes 196616 | tf_op jit(solution)/shard_map/ppermute | solution.py:20
  56.4 3.4 %collective-permute-done.7 = f32[128,128]{1,0:T(8,128)S(1)} collective-permute-done((f32[128,128]{1,0:T(8,128)S(1)}, f32[128,128]{1,0:T(8,128)S(1)}, u32[]{:S(2)}, u32[]{:S(2)}) %collective-permute-start.7) | collective-permute-done | bytes 65568 | tf_op jit(solution)/shard_map/ppermute | solution.py:20
  62.0 3.6 %collective-permute-start.8 = (f32[128,128]{1,0:T(8,128)S(1)}, f32[128,128]{1,0:T(8,128)S(1)}, u32[]{:S(2)}, u32[]{:S(2)}) collective-permute-start(f32[128,128]{1,0:T(8,128)S(1)} %get-tuple-element.45), channel_id=1, source_target_pairs={{0,4},{4,8},{8,12},{12,16},{16,20},{20,24},{24,28},{1,5},{5,9},{9,... | collective-permute-start | bytes 196616 | tf_op jit(solution)/shard_map/ppermute | solution.py:20
  65.7 2.5 %collective-permute-start.9 = (f32[128,128]{1,0:T(8,128)S(1)}, f32[128,128]{1,0:T(8,128)S(1)}, u32[]{:S(2)}, u32[]{:S(2)}) collective-permute-start(f32[128,128]{1,0:T(8,128)S(1)} %get-tuple-element.44), channel_id=1, source_target_pairs={{4,0},{8,4},{12,8},{16,12},{20,16},{24,20},{28,24},{5,1},{9,5},{13... | collective-permute-start | bytes 196616 | tf_op jit(solution)/shard_map/ppermute | solution.py:20
  68.2 2.4 %collective-permute-start.10 = (f32[128,128]{1,0:T(8,128)S(1)}, f32[128,128]{1,0:T(8,128)S(1)}, u32[]{:S(2)}, u32[]{:S(2)}) collective-permute-start(f32[128,128]{1,0:T(8,128)S(1)} %get-tuple-element.43), channel_id=1, source_target_pairs={{0,1},{1,2},{2,3},{4,5},{5,6},{6,7},{8,9},{9,10},{10,11},{12,13},{... | collective-permute-start | bytes 196616 | tf_op jit(solution)/shard_map/ppermute | solution.py:20
  72.6 3.6 %collective-permute-done.11 = f32[128,128]{1,0:T(8,128)S(1)} collective-permute-done((f32[128,128]{1,0:T(8,128)S(1)}, f32[128,128]{1,0:T(8,128)S(1)}, u32[]{:S(2)}, u32[]{:S(2)}) %collective-permute-start.11) | collective-permute-done | bytes 65568 | tf_op jit(solution)/shard_map/ppermute | solution.py:20
  78.4 2.7 %collective-permute-start.12 = (f32[128,128]{1,0:T(8,128)S(1)}, f32[128,128]{1,0:T(8,128)S(1)}, u32[]{:S(2)}, u32[]{:S(2)}) collective-permute-start(f32[128,128]{1,0:T(8,128)S(1)} %get-tuple-element.41), channel_id=1, source_target_pairs={{0,4},{4,8},{8,12},{12,16},{16,20},{20,24},{24,28},{1,5},{5,9},{9,... | collective-permute-start | bytes 196616 | tf_op jit(solution)/shard_map/ppermute | solution.py:20
  81.2 3.4 %collective-permute-start.13 = (f32[128,128]{1,0:T(8,128)S(1)}, f32[128,128]{1,0:T(8,128)S(1)}, u32[]{:S(2)}, u32[]{:S(2)}) collective-permute-start(f32[128,128]{1,0:T(8,128)S(1)} %get-tuple-element.40), channel_id=1, source_target_pairs={{4,0},{8,4},{12,8},{16,12},{20,16},{24,20},{28,24},{5,1},{9,5},{13... | collective-permute-start | bytes 196616 | tf_op jit(solution)/shard_map/ppermute | solution.py:20
  84.6 2.4 %collective-permute-start.14 = (f32[128,128]{1,0:T(8,128)S(1)}, f32[128,128]{1,0:T(8,128)S(1)}, u32[]{:S(2)}, u32[]{:S(2)}) collective-permute-start(f32[128,128]{1,0:T(8,128)S(1)} %get-tuple-element.39), channel_id=1, source_target_pairs={{0,1},{1,2},{2,3},{4,5},{5,6},{6,7},{8,9},{9,10},{10,11},{12,13},{... | collective-permute-start | bytes 196616 | tf_op jit(solution)/shard_map/ppermute | solution.py:20
  89.0 3.6 %collective-permute-done.15 = f32[128,128]{1,0:T(8,128)S(1)} collective-permute-done((f32[128,128]{1,0:T(8,128)S(1)}, f32[128,128]{1,0:T(8,128)S(1)}, u32[]{:S(2)}, u32[]{:S(2)}) %collective-permute-start.15) | collective-permute-done | bytes 65568 | tf_op jit(solution)/shard_map/ppermute | solution.py:20
  92.7 2.8 %fusion.56 = f32[1,1,768,128]{3,2,1,0:T(8,128)} fusion(f32[768,128]{1,0:T(8,128)S(1)} %fusion.57, f32[768,768]{1,0:T(8,128)S(1)} %fusion.46, f32[768,128]{1,0:T(8,128)S(1)} %fusion.54, f32[1,1,768,128]{3,2,1,0:T(8,128)S(1)} %copy-done), kind=kOutput, calls=%fused_computation.49 | convolution fusion | flops 906166272 | bytes 3932160 | tf_op jit(solution)/shard_map/dot_general | solution.py:33
  (57 shorter events, 20.7 us)
Async XLA Ops:
  2.3 33.8 %collective-permute-start = (f32[128,128]{1,0:T(8,128)}, f32[128,128]{1,0:T(8,128)}, u32[]{:S(2)}, u32[]{:S(2)}) collective-permute-start(f32[128,128]{1,0:T(8,128)} %get-tuple-element.52), channel_id=1, source_target_pairs={{0,4},{4,8},{8,12},{12,16},{16,20},{20,24},{24,28},{1,5},{5,9},{9,... | collective-permute-start | bytes 196616 | tf_op jit(solution)/shard_map/ppermute | solution.py:20
  5.4 31.5 %collective-permute-start.1 = (f32[128,128]{1,0:T(8,128)}, f32[128,128]{1,0:T(8,128)}, u32[]{:S(2)}, u32[]{:S(2)}) collective-permute-start(f32[128,128]{1,0:T(8,128)} %get-tuple-element.51), channel_id=1, source_target_pairs={{4,0},{8,4},{12,8},{16,12},{20,16},{24,20},{28,24},{5,1},{9,5},{13... | collective-permute-start | bytes 196616 | tf_op jit(solution)/shard_map/ppermute | solution.py:20
  8.4 29.3 %collective-permute-start.2 = (f32[128,128]{1,0:T(8,128)}, f32[128,128]{1,0:T(8,128)}, u32[]{:S(2)}, u32[]{:S(2)}) collective-permute-start(f32[128,128]{1,0:T(8,128)} %get-tuple-element.53), channel_id=1, source_target_pairs={{0,1},{1,2},{2,3},{4,5},{5,6},{6,7},{8,9},{9,10},{10,11},{12,13},{... | collective-permute-start | bytes 196616 | tf_op jit(solution)/shard_map/ppermute | solution.py:20
  12.7 25.9 %collective-permute-start.3 = (f32[128,128]{1,0:T(8,128)}, f32[128,128]{1,0:T(8,128)}, u32[]{:S(2)}, u32[]{:S(2)}) collective-permute-start(f32[128,128]{1,0:T(8,128)} %get-tuple-element.50), channel_id=1, source_target_pairs={{1,0},{2,1},{3,2},{5,4},{6,5},{7,6},{9,8},{10,9},{11,10},{13,12},{... | collective-permute-start | bytes 196616 | tf_op jit(solution)/shard_map/ppermute | solution.py:20
  30.5 1.7 %copy-start.3 = (bf16[1,1,768,768]{3,2,1,0:T(8,128)(2,1)S(1)}, bf16[1,1,768,768]{3,2,1,0:T(8,128)(2,1)}, u32[]{:S(2)}) copy-start(bf16[1,1,768,768]{3,2,1,0:T(8,128)(2,1)} %param.16) | copy-start | bytes 3538948
  32.2 7.2 %copy-start.2 = (f32[1,1,768,128]{3,2,1,0:T(8,128)S(1)}, f32[1,1,768,128]{3,2,1,0:T(8,128)}, u32[]{:S(2)}) copy-start(f32[1,1,768,128]{3,2,1,0:T(8,128)} %param.18) | copy-start | bytes 1179652
  32.2 7.3 %copy-start = (f32[1,1,768,128]{3,2,1,0:T(8,128)S(1)}, f32[1,1,768,128]{3,2,1,0:T(8,128)}, u32[]{:S(2)}) copy-start(f32[1,1,768,128]{3,2,1,0:T(8,128)} %param.19) | copy-start | bytes 1179652
  41.6 14.8 %collective-permute-start.4 = (f32[128,128]{1,0:T(8,128)S(1)}, f32[128,128]{1,0:T(8,128)S(1)}, u32[]{:S(2)}, u32[]{:S(2)}) collective-permute-start(f32[128,128]{1,0:T(8,128)S(1)} %get-tuple-element.49), channel_id=1, source_target_pairs={{0,4},{4,8},{8,12},{12,16},{16,20},{20,24},{24,28},{1,5},{5,9},{9,... | collective-permute-start | bytes 196616 | tf_op jit(solution)/shard_map/ppermute | solution.py:20
  44.5 11.9 %collective-permute-start.5 = (f32[128,128]{1,0:T(8,128)S(1)}, f32[128,128]{1,0:T(8,128)S(1)}, u32[]{:S(2)}, u32[]{:S(2)}) collective-permute-start(f32[128,128]{1,0:T(8,128)S(1)} %get-tuple-element.48), channel_id=1, source_target_pairs={{4,0},{8,4},{12,8},{16,12},{20,16},{24,20},{28,24},{5,1},{9,5},{13... | collective-permute-start | bytes 196616 | tf_op jit(solution)/shard_map/ppermute | solution.py:20
  47.8 8.6 %collective-permute-start.6 = (f32[128,128]{1,0:T(8,128)S(1)}, f32[128,128]{1,0:T(8,128)S(1)}, u32[]{:S(2)}, u32[]{:S(2)}) collective-permute-start(f32[128,128]{1,0:T(8,128)S(1)} %get-tuple-element.47), channel_id=1, source_target_pairs={{0,1},{1,2},{2,3},{4,5},{5,6},{6,7},{8,9},{9,10},{10,11},{12,13},{... | collective-permute-start | bytes 196616 | tf_op jit(solution)/shard_map/ppermute | solution.py:20
  54.2 5.6 %collective-permute-start.7 = (f32[128,128]{1,0:T(8,128)S(1)}, f32[128,128]{1,0:T(8,128)S(1)}, u32[]{:S(2)}, u32[]{:S(2)}) collective-permute-start(f32[128,128]{1,0:T(8,128)S(1)} %get-tuple-element.46), channel_id=1, source_target_pairs={{1,0},{2,1},{3,2},{5,4},{6,5},{7,6},{9,8},{10,9},{11,10},{13,12},{... | collective-permute-start | bytes 196616 | tf_op jit(solution)/shard_map/ppermute | solution.py:20
  62.0 10.6 %collective-permute-start.8 = (f32[128,128]{1,0:T(8,128)S(1)}, f32[128,128]{1,0:T(8,128)S(1)}, u32[]{:S(2)}, u32[]{:S(2)}) collective-permute-start(f32[128,128]{1,0:T(8,128)S(1)} %get-tuple-element.45), channel_id=1, source_target_pairs={{0,4},{4,8},{8,12},{12,16},{16,20},{20,24},{24,28},{1,5},{5,9},{9,... | collective-permute-start | bytes 196616 | tf_op jit(solution)/shard_map/ppermute | solution.py:20
  65.7 6.9 %collective-permute-start.9 = (f32[128,128]{1,0:T(8,128)S(1)}, f32[128,128]{1,0:T(8,128)S(1)}, u32[]{:S(2)}, u32[]{:S(2)}) collective-permute-start(f32[128,128]{1,0:T(8,128)S(1)} %get-tuple-element.44), channel_id=1, source_target_pairs={{4,0},{8,4},{12,8},{16,12},{20,16},{24,20},{28,24},{5,1},{9,5},{13... | collective-permute-start | bytes 196616 | tf_op jit(solution)/shard_map/ppermute | solution.py:20
  68.2 4.4 %collective-permute-start.10 = (f32[128,128]{1,0:T(8,128)S(1)}, f32[128,128]{1,0:T(8,128)S(1)}, u32[]{:S(2)}, u32[]{:S(2)}) collective-permute-start(f32[128,128]{1,0:T(8,128)S(1)} %get-tuple-element.43), channel_id=1, source_target_pairs={{0,1},{1,2},{2,3},{4,5},{5,6},{6,7},{8,9},{9,10},{10,11},{12,13},{... | collective-permute-start | bytes 196616 | tf_op jit(solution)/shard_map/ppermute | solution.py:20
  70.6 5.6 %collective-permute-start.11 = (f32[128,128]{1,0:T(8,128)S(1)}, f32[128,128]{1,0:T(8,128)S(1)}, u32[]{:S(2)}, u32[]{:S(2)}) collective-permute-start(f32[128,128]{1,0:T(8,128)S(1)} %get-tuple-element.42), channel_id=1, source_target_pairs={{1,0},{2,1},{3,2},{5,4},{6,5},{7,6},{9,8},{10,9},{11,10},{13,12},{... | collective-permute-start | bytes 196616 | tf_op jit(solution)/shard_map/ppermute | solution.py:20
  78.4 17.1 %copy-start.1 = (f32[768,128]{1,0:T(8,128)}, f32[768,128]{1,0:T(8,128)S(1)}, u32[]{:S(2)}) copy-start(f32[768,128]{1,0:T(8,128)S(1)} %fusion.54) | copy-start | bytes 1179652
  78.4 10.6 %collective-permute-start.12 = (f32[128,128]{1,0:T(8,128)S(1)}, f32[128,128]{1,0:T(8,128)S(1)}, u32[]{:S(2)}, u32[]{:S(2)}) collective-permute-start(f32[128,128]{1,0:T(8,128)S(1)} %get-tuple-element.41), channel_id=1, source_target_pairs={{0,4},{4,8},{8,12},{12,16},{16,20},{20,24},{24,28},{1,5},{5,9},{9,... | collective-permute-start | bytes 196616 | tf_op jit(solution)/shard_map/ppermute | solution.py:20
  81.2 7.8 %collective-permute-start.13 = (f32[128,128]{1,0:T(8,128)S(1)}, f32[128,128]{1,0:T(8,128)S(1)}, u32[]{:S(2)}, u32[]{:S(2)}) collective-permute-start(f32[128,128]{1,0:T(8,128)S(1)} %get-tuple-element.40), channel_id=1, source_target_pairs={{4,0},{8,4},{12,8},{16,12},{20,16},{24,20},{28,24},{5,1},{9,5},{13... | collective-permute-start | bytes 196616 | tf_op jit(solution)/shard_map/ppermute | solution.py:20
  84.6 4.4 %collective-permute-start.14 = (f32[128,128]{1,0:T(8,128)S(1)}, f32[128,128]{1,0:T(8,128)S(1)}, u32[]{:S(2)}, u32[]{:S(2)}) collective-permute-start(f32[128,128]{1,0:T(8,128)S(1)} %get-tuple-element.39), channel_id=1, source_target_pairs={{0,1},{1,2},{2,3},{4,5},{5,6},{6,7},{8,9},{9,10},{10,11},{12,13},{... | collective-permute-start | bytes 196616 | tf_op jit(solution)/shard_map/ppermute | solution.py:20
  87.0 5.6 %collective-permute-start.15 = (f32[128,128]{1,0:T(8,128)S(1)}, f32[128,128]{1,0:T(8,128)S(1)}, u32[]{:S(2)}, u32[]{:S(2)}) collective-permute-start(f32[128,128]{1,0:T(8,128)S(1)} %get-tuple-element.38), channel_id=1, source_target_pairs={{1,0},{2,1},{3,2},{5,4},{6,5},{7,6},{9,8},{10,9},{11,10},{13,12},{... | collective-permute-start | bytes 196616 | tf_op jit(solution)/shard_map/ppermute | solution.py:20
where the time goes:
time: 97.1 us; the launch traced here: 95.5 us
  starting transfers between devices  48.1 us (50%)
  matrix products  24.1 us (25%)
  waiting for transfers between devices  10.6 us (11%)
  local copies, waits for them, and re-layouts  6.92 us (7%)
  other arithmetic  4.04 us (4%)
  between operations  1.67 us (2%)
    ppermute x16, starting transfers between devices, from_behind(): return lax.ppermute(block, axis, route)  48.1 us
    dot_general x3, matrix products, schur_block(): jnp.dot(product, coupling_block.T, preferred_element_type=jnp.float32)  15.2 us
    ppermute x16, waiting for transfers between devices, from_behind(): return lax.ppermute(block, axis, route)  10.6 us
    dot_general x4, matrix products, apply_operator(): jnp.dot(condensed, traces, precision=lax.Precision.HIGHEST, preferred_ele...  8.94 us
    sub x1, other arithmetic, on_device(): condensed = condensed - term  3.82 us
    unnamed x24, local copies, waits for them, and re-layouts  3.58 us
  transfers between devices with their start and end apart: 16, of which 3 were waited for; matrix products, arithmetic and copies ran while one was open for 24% of the time, Pallas kernels for 0%

commit v1 on v0

v1 whole, which is shorter than its diff:
```python
import functools

import jax
import jax.numpy as jnp
from jax import lax
from jax.experimental import pallas as pl
from jax.experimental.pallas import tpu as pltpu
from jax.sharding import PartitionSpec as P

SWEEPS = 3
FACES = 6

penalty_weight = 2.0
lower_bound = 1.0
upper_bound = 14.0
spectrum_centre = (upper_bound + lower_bound) / 2.0
spectrum_half = (upper_bound - lower_bound) / 2.0
sigma_ratio = spectrum_centre / spectrum_half


def sweep_weights():
    weights = [(0.0, 1.0 / spectrum_centre)]
    weight_old = 1.0 / sigma_ratio
    for _ in range(SWEEPS - 1):
        weight_new = 1.0 / (2.0 * sigma_ratio - weight_old)
        weights.append((weight_new * weight_old, 2.0 * weight_new / spectrum_half))
        weight_old = weight_new
    return weights


def two_parts(value):
    high = value.astype(jnp.bfloat16)
    low = (value - high.astype(jnp.float32)).astype(jnp.bfloat16)
    return high, low


def product(left, right, dims):
    return lax.dot_general(left, right, (dims, ((), ())), preferred_element_type=jnp.float32)


def kernel(
    axis_sizes,
    coupling,
    inverse,
    stiffness,
    live,
    initial,
    loads,
    traces_out,
    residual_out,
    wide,
    inv,
    factors,
    turned,
    inner,
    held,
    bound,
    direction,
    landed,
    in_sems,
    send_sems,
    recv_sems,
):
    slots, trace_width, inner_width = coupling.shape
    load_width = initial.shape[1]
    mode_width = trace_width // FACES
    rows, groups, halves = axis_sizes
    columns = groups * halves
    row = lax.axis_index("gx")
    column = lax.axis_index("gy") * halves + lax.axis_index("ha")

    def column_id(index):
        return {"gy": lax.div(index, halves), "ha": lax.rem(index, halves)}

    routes = (
        (1, 0, row + 1 < rows, {"gx": row + 1}),
        (0, 1, row > 0, {"gx": row - 1}),
        (3, 2, column + 1 < columns, column_id(column + 1)),
        (2, 3, column > 0, column_id(column - 1)),
    )
    arrivals = ((0, row > 0), (1, row + 1 < rows), (2, column > 0), (3, column + 1 < columns))

    copies = [
        pltpu.make_async_copy(initial, held, in_sems.at[0]),
        pltpu.make_async_copy(loads, bound, in_sems.at[1]),
        pltpu.make_async_copy(stiffness, wide.at[:, pl.ds(0, trace_width)], in_sems.at[2]),
    ]
    coupling_copies, inverse_copies = [], []
    for slot in range(slots):
        spot = pl.ds(trace_width + slot * inner_width, inner_width)
        coupling_copies.append(
            pltpu.make_async_copy(coupling.at[slot], wide.at[:, spot], in_sems.at[3 + slot])
        )
        inverse_copies.append(
            pltpu.make_async_copy(inverse.at[slot], inv.at[slot], in_sems.at[3 + slots + slot])
        )
    copies[0].start()
    for slot in range(slots):
        coupling_copies[slot].start()
        inverse_copies[slot].start()
    copies[2].start()
    copies[1].start()

    barrier = pltpu.get_barrier_semaphore()
    partners = 0
    for _, _, exists, target in routes:
        partners = partners + exists.astype(jnp.int32)

        @pl.when(exists)
        def _():
            pl.semaphore_signal(barrier, inc=1, device_id=target, device_id_type=pl.DeviceIdType.MESH)

    for face, exists in arrivals:

        @pl.when(jnp.logical_not(exists))
        def _():
            landed[:, face] = jnp.zeros((SWEEPS + 1, mode_width, load_width), jnp.float32)

    pl.semaphore_wait(barrier, partners)

    def outgoing(step, route):
        face, spot, _, target = route
        return pltpu.make_async_remote_copy(
            src_ref=held.at[pl.ds(face * mode_width, mode_width)],
            dst_ref=landed.at[step, spot],
            send_sem=send_sems.at[face],
            recv_sem=recv_sems.at[step, spot],
            device_id=target,
            device_id_type=pl.DeviceIdType.MESH,
        )

    def send(step, route):
        @pl.when(route[2])
        def _():
            outgoing(step, route).start()

    def wait_sent(step):
        for route in routes:

            @pl.when(route[2])
            def _():
                outgoing(step, route).wait_send()

    def wait_arrived(step):
        for (face, exists), route in zip(arrivals, routes):

            @pl.when(exists)
            def _():
                outgoing(step, route).wait_recv()

    def keep_parts(traces):
        high, low = two_parts(traces)
        factors[pl.ds(0, trace_width), pl.ds(0, load_width)] = high
        factors[pl.ds(0, trace_width), pl.ds(load_width, load_width)] = low
        high, low = two_parts(traces.T)
        turned[pl.ds(0, load_width)] = high
        turned[pl.ds(load_width, load_width)] = low

    def apply(first):
        for slot in range(slots):
            spot = pl.ds(trace_width + slot * inner_width, inner_width)
            if first:
                coupling_copies[slot].wait()
            both = product(turned[...], wide[:, spot], ((1,), (0,)))
            high, low = two_parts(both[:load_width] + both[load_width:])
            inner[slot, pl.ds(0, load_width)] = high
            inner[slot, pl.ds(load_width, load_width)] = low
        for slot in range(slots):
            spot = pl.ds(trace_width + slot * inner_width, inner_width)
            if first:
                inverse_copies[slot].wait()
            both = product(inv[slot], inner[slot], ((1,), (1,)))
            high, low = two_parts((both[:, :load_width] + both[:, load_width:]) * live[slot])
            factors[spot, pl.ds(0, load_width)] = high
            factors[spot, pl.ds(load_width, load_width)] = low
        if first:
            copies[2].wait()
        both = product(wide[...], factors[...], ((1,), (0,)))
        return both[:, :load_width] + both[:, load_width:]

    def residual_of(step, coupled):
        residual_out[...] = bound[...] - coupled - penalty_weight * held[...]
        wait_arrived(step)
        for face in range(4):
            spot = pl.ds(face * mode_width, mode_width)
            residual_out[spot] = residual_out[spot] + penalty_weight * landed[step, face]

    def advance(step, old_weight, new_weight):
        wait_sent(step)
        change = new_weight * residual_out[...]
        if old_weight is not None:
            change = change + old_weight * direction[...]
        direction[...] = change
        traces = held[...] + change
        held[...] = traces
        for route in routes:
            send(step + 1, route)
        keep_parts(held[...])

    weights = sweep_weights()

    copies[0].wait()
    for route in routes:
        send(0, route)
    keep_parts(held[...])
    coupled = apply(True)
    copies[1].wait()
    residual_of(0, coupled)
    advance(0, None, weights[0][1])

    def sweep(step, carry):
        residual_of(step, apply(False))

        @pl.when(step < SWEEPS)
        def _():
            old_weight, new_weight = weights[-1]
            for index in range(SWEEPS - 1, 0, -1):
                old_weight = jnp.where(step == index, weights[index][0], old_weight)
                new_weight = jnp.where(step == index, weights[index][1], new_weight)
            advance(step, old_weight, new_weight)

        return carry

    lax.fori_loop(1, SWEEPS + 1, sweep, 0)
    wait_sent(SWEEPS)
    traces_out[...] = held[...]


def on_device(
    axis_sizes, coupling, interior_inverse, boundary_stiffness, block_counts, initial_traces, trace_loads
):
    slots, trace_width, inner_width = coupling.shape[2:]
    load_width = initial_traces.shape[-1]
    mode_width = trace_width // FACES
    live = jnp.where(jnp.arange(slots) < block_counts[0, 0], -1.0, 0.0).astype(jnp.float32)
    whole = pl.BlockSpec(memory_space=pl.ANY)
    out = jax.ShapeDtypeStruct((trace_width, load_width), jnp.float32)
    wide_width = trace_width + slots * inner_width
    traces, residual = pl.pallas_call(
        functools.partial(kernel, axis_sizes),
        out_shape=(out, out),
        in_specs=[whole, whole, whole, pl.BlockSpec(memory_space=pltpu.SMEM), whole, whole],
        out_specs=(pl.BlockSpec(memory_space=pltpu.VMEM),) * 2,
        scratch_shapes=[
            pltpu.VMEM((trace_width, wide_width), jnp.bfloat16),
            pltpu.VMEM((slots, inner_width, inner_width), jnp.bfloat16),
            pltpu.VMEM((wide_width, 2 * load_width), jnp.bfloat16),
            pltpu.VMEM((2 * load_width, trace_width), jnp.bfloat16),
            pltpu.VMEM((slots, 2 * load_width, inner_width), jnp.bfloat16),
            pltpu.VMEM((trace_width, load_width), jnp.float32),
            pltpu.VMEM((trace_width, load_width), jnp.float32),
            pltpu.VMEM((trace_width, load_width), jnp.float32),
            pltpu.VMEM((SWEEPS + 1, 4, mode_width, load_width), jnp.float32),
            pltpu.SemaphoreType.DMA((3 + 2 * slots,)),
            pltpu.SemaphoreType.DMA((4,)),
            pltpu.SemaphoreType.DMA((SWEEPS + 1, 4)),
        ],
        compiler_params=pltpu.CompilerParams(
            collective_id=0, has_side_effects=True, vmem_limit_bytes=48 << 20
        ),
        name="condense_and_sweep",
    )(
        coupling[0, 0],
        interior_inverse[0, 0],
        boundary_stiffness[0, 0],
        live,
        initial_traces[0, 0],
        trace_loads[0, 0],
    )
    return (traces[None, None], residual[None, None])


def solution(mesh):
    in_specs = (
        P("gx", ("gy", "ha"), None, None, None),
        P("gx", ("gy", "ha"), None, None, None),
        P("gx", ("gy", "ha"), None, None),
        P("gx", ("gy", "ha")),
        P("gx", ("gy", "ha"), None, None),
        P("gx", ("gy", "ha"), None, None),
    )
    out_specs = (P("gx", ("gy", "ha"), None, None), P("gx", ("gy", "ha"), None, None))
    axis_sizes = (mesh.shape["gx"], mesh.shape["gy"], mesh.shape["ha"])
    return jax.shard_map(
        functools.partial(on_device, axis_sizes),
        mesh=mesh, in_specs=in_specs, out_specs=out_specs, check_vma=False,
    )
```

time: 97.1 us -> 34.2 us (0.35)
  the two profiles are of different devices: /device:TPU:25 before, /device:TPU:0 now
where the time goes in v1:
time: 34.2 us; the launch traced here: 33.9 us
  Pallas kernels  27.9 us (82%)
  local copies, waits for them, and re-layouts  4.75 us (14%)
  between operations  1.3 us (4%)
    pallas_call x1, Pallas kernels, on_device(): pl.pallas_call(functools.partial(kernel, axis_sizes), out_shape=(out, out...  27.9 us
    unnamed x8, local copies, waits for them, and re-layouts  4.75 us

profile of v1, /device:TPU:0, one launch (start us, length us, event | category | flops | bytes accessed | tf_op | source)
XLA Modules:
  0.0 33.9 jit_solution(1306837084707795723)
XLA Ops:
  1.3 0.0 copy-start
  1.3 1.3 %copy-done = bf16[1,1,768,768]{3,2,1,0:T(8,128)(2,1)S(1)} copy-done((bf16[1,1,768,768]{3,2,1,0:T(8,128)(2,1)S(1)}, bf16[1,1,768,768]{3,2,1,0:T(8,128)(2,1)}, u32[]{:S(2)}) %copy-start) | copy-done | bytes 1179672
  2.6 0.0 copy-start.1
  2.6 1.0 %copy-done.1 = f32[1,1,768,128]{3,2,1,0:T(8,128)S(1)} copy-done((f32[1,1,768,128]{3,2,1,0:T(8,128)S(1)}, f32[1,1,768,128]{3,2,1,0:T(8,128)}, u32[]{:S(2)}) %copy-start.1) | copy-done | bytes 393240
  3.6 0.0 copy-start.2
  3.6 1.0 %copy-done.2 = f32[1,1,768,128]{3,2,1,0:T(8,128)S(1)} copy-done((f32[1,1,768,128]{3,2,1,0:T(8,128)S(1)}, f32[1,1,768,128]{3,2,1,0:T(8,128)}, u32[]{:S(2)}) %copy-start.2) | copy-done | bytes 393240
  4.6 27.9 %condense_and_sweep.1 = (f32[768,128]{1,0:T(8,128)S(1)}, f32[768,128]{1,0:T(8,128)S(1)}) custom-call(bf16[4,768,768]{2,1,0:T(8,128)(2,1)} %bitcast.14, bf16[4,768,768]{2,1,0:T(8,128)(2,1)} %bitcast.15, bf16[768,768]{1,0:T(8,128)(2,1)S(1)} %bitcast.9, f32[4]{0:T(128)S(1)} %compare_select_fusion.live, f32[768,128]{1,0:T(8,128)S(1)} %bitcast.10, ...), custom_call_target="tpu_custom_call" | custom-call | tf_op jit(solution)/shard_map/condense_and_sweep/pallas_call | solution.py:239
  32.4 0.7 %copy.11 = f32[1,1,768,128]{3,2,1,0:T(8,128)} copy(f32[1,1,768,128]{3,2,1,0:T(8,128)S(1)} %bitcast.13) | data formatting | bytes 786432
  33.2 0.7 %copy.12 = f32[1,1,768,128]{3,2,1,0:T(8,128)} copy(f32[1,1,768,128]{3,2,1,0:T(8,128)S(1)} %bitcast.12) | data formatting | bytes 786432
  (1 shorter events, 0.0 us)
Async XLA Ops:
  1.3 1.3 %copy-start = (bf16[1,1,768,768]{3,2,1,0:T(8,128)(2,1)S(1)}, bf16[1,1,768,768]{3,2,1,0:T(8,128)(2,1)}, u32[]{:S(2)}) copy-start(bf16[1,1,768,768]{3,2,1,0:T(8,128)(2,1)} %param.8) | copy-start | bytes 3538948
  2.6 1.0 %copy-start.1 = (f32[1,1,768,128]{3,2,1,0:T(8,128)S(1)}, f32[1,1,768,128]{3,2,1,0:T(8,128)}, u32[]{:S(2)}) copy-start(f32[1,1,768,128]{3,2,1,0:T(8,128)} %param.10) | copy-start | bytes 1179652
  3.6 1.0 %copy-start.2 = (f32[1,1,768,128]{3,2,1,0:T(8,128)S(1)}, f32[1,1,768,128]{3,2,1,0:T(8,128)}, u32[]{:S(2)}) copy-start(f32[1,1,768,128]{3,2,1,0:T(8,128)} %param.11) | copy-start | bytes 1179652

commit v2 on v1

--- a/solution.py
+++ b/solution.py
@@ -43,7 +43,7 @@
     coupling,
     inverse,
     stiffness,
-    live,
+    counts,
     initial,
     loads,
     traces_out,
@@ -95,9 +95,8 @@
             pltpu.make_async_copy(inverse.at[slot], inv.at[slot], in_sems.at[3 + slots + slot])
         )
     copies[0].start()
-    for slot in range(slots):
-        coupling_copies[slot].start()
-        inverse_copies[slot].start()
+    for copy in coupling_copies + inverse_copies:
+        copy.start()
     copies[2].start()
     copies[1].start()
 
@@ -157,24 +156,29 @@
         turned[pl.ds(load_width, load_width)] = low
 
     def apply(first):
+        @pl.when(first)
+        def _():
+            for copy in coupling_copies:
+                copy.wait()
+
         for slot in range(slots):
             spot = pl.ds(trace_width + slot * inner_width, inner_width)
-            if first:
-                coupling_copies[slot].wait()
             both = product(turned[...], wide[:, spot], ((1,), (0,)))
             high, low = two_parts(both[:load_width] + both[load_width:])
             inner[slot, pl.ds(0, load_width)] = high
             inner[slot, pl.ds(load_width, load_width)] = low
+
+        @pl.when(first)
+        def _():
+            for copy in inverse_copies + copies[1:]:
+                copy.wait()
+
         for slot in range(slots):
             spot = pl.ds(trace_width + slot * inner_width, inner_width)
-            if first:
-                inverse_copies[slot].wait()
             both = product(inv[slot], inner[slot], ((1,), (1,)))
-            high, low = two_parts((both[:, :load_width] + both[:, load_width:]) * live[slot])
+            high, low = two_parts((both[:, :load_width] + both[:, load_width:]) * jnp.where(counts[0, 0] > slot, -1.0, 0.0))
             factors[spot, pl.ds(0, load_width)] = high
             factors[spot, pl.ds(load_width, load_width)] = low
-        if first:
-            copies[2].wait()
         both = product(wide[...], factors[...], ((1,), (0,)))
         return both[:, :load_width] + both[:, load_width:]
 
@@ -187,9 +191,7 @@
 
     def advance(step, old_weight, new_weight):
         wait_sent(step)
-        change = new_weight * residual_out[...]
-        if old_weight is not None:
-            change = change + old_weight * direction[...]
+        change = new_weight * residual_out[...] + old_weight * direction[...]
         direction[...] = change
         traces = held[...] + change
         held[...] = traces
@@ -203,25 +205,22 @@
     for route in routes:
         send(0, route)
     keep_parts(held[...])
-    coupled = apply(True)
-    copies[1].wait()
-    residual_of(0, coupled)
-    advance(0, None, weights[0][1])
+    direction[...] = jnp.zeros_like(direction)
 
     def sweep(step, carry):
-        residual_of(step, apply(False))
+        residual_of(step, apply(step == 0))
 
         @pl.when(step < SWEEPS)
         def _():
             old_weight, new_weight = weights[-1]
-            for index in range(SWEEPS - 1, 0, -1):
+            for index in range(SWEEPS - 1):
                 old_weight = jnp.where(step == index, weights[index][0], old_weight)
                 new_weight = jnp.where(step == index, weights[index][1], new_weight)
             advance(step, old_weight, new_weight)
 
         return carry
 
-    lax.fori_loop(1, SWEEPS + 1, sweep, 0)
+    lax.fori_loop(0, SWEEPS + 1, sweep, 0)
     wait_sent(SWEEPS)
     traces_out[...] = held[...]
 
@@ -232,8 +231,7 @@
     slots, trace_width, inner_width = coupling.shape[2:]
     load_width = initial_traces.shape[-1]
     mode_width = trace_width // FACES
-    live = jnp.where(jnp.arange(slots) < block_counts[0, 0], -1.0, 0.0).astype(jnp.float32)
-    whole = pl.BlockSpec(memory_space=pl.ANY)
+    whole = pl.BlockSpec(memory_space=pltpu.HBM)
     out = jax.ShapeDtypeStruct((trace_width, load_width), jnp.float32)
     wide_width = trace_width + slots * inner_width
     traces, residual = pl.pallas_call(
@@ -256,14 +254,14 @@
             pltpu.SemaphoreType.DMA((SWEEPS + 1, 4)),
         ],
         compiler_params=pltpu.CompilerParams(
-            collective_id=0, has_side_effects=True, vmem_limit_bytes=48 << 20
+            collective_id=0, has_side_effects=True, vmem_limit_bytes=67043328
         ),
         name="condense_and_sweep",
     )(
         coupling[0, 0],
         interior_inverse[0, 0],
         boundary_stiffness[0, 0],
-        live,
+        block_counts,
         initial_traces[0, 0],
         trace_loads[0, 0],
     )

time: 34.2 us -> 29.7 us (0.87)
  Pallas kernels: 27.9 us -> 24.7 us
  local copies, waits for them, and re-layouts: 4.75 us -> 3.53 us
    pallas_call x1, Pallas kernels: 27.9 us -> 24.7 us  [on_device(): pl.pallas_call(functools.partial(kernel, axis_sizes), out_shape=(out, out...]
    unnamed x8 -> x2, local copies, waits for them, and re-layouts: 4.75 us -> 3.53 us
where the time goes in v2:
time: 29.7 us; the launch traced here: 29.5 us
  Pallas kernels  24.7 us (83%)
  local copies, waits for them, and re-layouts  3.53 us (12%)
  between operations  1.29 us (4%)
    pallas_call x1, Pallas kernels, on_device(): pl.pallas_call(functools.partial(kernel, axis_sizes), out_shape=(out, out...  24.7 us
    unnamed x2, local copies, waits for them, and re-layouts  3.53 us

profile of v2, /device:TPU:0, one launch (start us, length us, event | category | flops | bytes accessed | tf_op | source)
XLA Modules:
  0.0 29.5 jit_solution(2529162496017982665)
XLA Ops:
  1.3 24.7 %condense_and_sweep.1 = (f32[768,128]{1,0:T(8,128)}, f32[768,128]{1,0:T(8,128)}) custom-call(bf16[4,768,768]{2,1,0:T(8,128)(2,1)} %bitcast.7, bf16[4,768,768]{2,1,0:T(8,128)(2,1)} %bitcast.8, bf16[768,768]{1,0:T(8,128)(2,1)} %bitcast.9, s32[1,1]{1,0:T(1,128)S(6)} %copy.10.counts, f32[768,128]{1,0:T(8,128)} %bitcast.10, f32[768,128]{1,0:T(8,128)} %bitcast.11), custom_call_target="tpu_custom_call" | custom-call | tf_op jit(solution)/shard_map/condense_and_sweep/pallas_call | solution.py:237
  26.0 1.8 %copy.11 = f32[1,1,768,128]{3,2,1,0:T(8,128)} copy(f32[1,1,768,128]{3,2,1,0:T(8,128)} %bitcast.13) | data formatting | bytes 786432
  27.7 1.8 %copy.12 = f32[1,1,768,128]{3,2,1,0:T(8,128)} copy(f32[1,1,768,128]{3,2,1,0:T(8,128)} %bitcast.12) | data formatting | bytes 786432
